TPU v7x, 32 devices: a whole 2x2x4 slice. The times are simulated.
32 devices in a mesh: seq: 4 (over y, x), tp: 8 (over z, core).
Axes of the slice: x: 2, y: 2, z: 4, core: 2. Of those that a mesh axis runs over, the one named last changes fastest.
Arguments:
- tokens: bfloat16 [1024, 4096], P('seq', 'tp'), may hold values from -30 to 30
- w_qkv: bfloat16 [4096, 3, 2048], P('seq', None, 'tp'), may hold values from -1 to 1
- keep_list: int32 [512], P('seq'), may hold values from 0 to 255, as said below
- counts: int32 [4], P('seq'), may hold values from 1 to 127, as said below
Outputs:
- attended: bfloat16 [256, 2048], P('seq', 'tp')
Inputs may be any that keep to these rules, and one draw needn't show every extreme that they name: `counts`: the entries sum to 256; one shard keeps 2 * 64 - 1 tokens and one shard keeps 1. `keep_list`: entries s * 2 * 64 to s * 2 * 64 + 2 * 64 - 1 are distinct token indices within shard s; the first counts[s] of them increase.
All inputs are finite; a program needn't handle non-finite values.
Results may differ from a plain program's by a relative error of at most 0.0065.
Values may be sent and summed in bfloat16 or wider, within the bound.
No kernel may reach another device: no remote copies, remote signals or barrier semaphores. Data moves between devices by JAX's collectives and lax.ppermute only.
A program may use at most 64 MiB of HBM per device.

v0:
```python
import jax
import jax.numpy as jnp
from jax import lax
from jax.sharding import PartitionSpec as P

HD = 128


def entering(value, axis, join, neutral):
    count, mine = (lax.axis_size(axis), lax.axis_index(axis))
    pieces = lax.all_gather(value, axis)
    so_far = jnp.full_like(value, 0) + jnp.asarray(neutral, value.dtype)

    def lap(position, so_far):
        longer = join(so_far, pieces[position])
        return jnp.where(position < mine, longer, so_far)

    return lax.fori_loop(0, count - 1, lap, so_far)


def add_sums(earlier, later):
    return earlier + later


def on_device(tokens, w_qkv, keep_list, counts):
    shards = lax.axis_size("seq")
    my_index = lax.axis_index("seq")
    tok_dev = tokens.shape[0]
    slots = keep_list.shape[0]
    capacity = slots // 2
    per_peer = slots // shards
    head_dim = HD
    columns = w_qkv.shape[2]
    local_heads = columns // head_dim
    offset = entering(counts, "seq", add_sums, jnp.zeros_like(counts))[0]
    peers = jnp.arange(shards, dtype=jnp.int32)[:, None]
    rounds = jnp.arange(per_peer, dtype=jnp.int32)[None, :]
    local_slot = (peers - offset) % shards + rounds * shards
    live = local_slot < counts[0]
    token_index = keep_list[local_slot]
    ranks = jnp.where(live, offset + local_slot, -1).astype(jnp.int32)
    positions = my_index * tok_dev + token_index
    meta = jnp.stack([positions, ranks], axis=2)
    picked = jnp.where(live[:, :, None], tokens[token_index], jnp.zeros((), tokens.dtype))
    arrived, arrived_meta = (
        lax.all_to_all(picked, "seq", split_axis=0, concat_axis=0, tiled=True),
        lax.all_to_all(meta, "seq", split_axis=0, concat_axis=0, tiled=True),
    )
    arrived_meta = arrived_meta.reshape(shards * per_peer, 2)
    arrived_rank = arrived_meta[:, 1]
    target = jnp.where(arrived_rank >= 0, arrived_rank // shards, capacity)
    flat = arrived.reshape(shards * per_peer, arrived.shape[2])
    kept = jnp.zeros((capacity, flat.shape[1]), flat.dtype).at[target].set(flat, mode="drop")
    kept_pos = jnp.zeros((capacity,), jnp.int32).at[target].set(arrived_meta[:, 0], mode="drop")
    full_rows = lax.all_gather(kept, "tp", axis=1, tiled=True)
    piece = lax.all_gather(w_qkv, "seq", axis=0, tiled=True)
    part_rows = lax.slice_in_dim(full_rows, 0, piece.shape[0], axis=1)
    projected = jnp.einsum(
        "rd,dgc->rgc", part_rows, piece, preferred_element_type=jnp.float32
    ).astype(jnp.bfloat16)
    queries = projected[:, 0].reshape(capacity, local_heads, head_dim)
    key_values = projected[:, 1:]
    scale = head_dim ** (-0.5)
    all_kv, all_pos = (
        lax.all_gather(key_values, "seq", axis=0, tiled=True),
        lax.all_gather(kept_pos, "seq", axis=0, tiled=True),
    )
    total_keys = all_kv.shape[0]
    keys_all = all_kv[:, 0].reshape(total_keys, local_heads, head_dim)
    values_all = all_kv[:, 1].reshape(total_keys, local_heads, head_dim)
    scores = (
        jnp.einsum("qhd,khd->hqk", queries, keys_all, preferred_element_type=jnp.float32) * scale
    )
    masked = all_pos[None, None, :] > kept_pos[None, :, None]
    scores = jnp.where(masked, -jnp.inf, scores)
    top = jnp.max(scores, axis=2, keepdims=True)
    expo = jnp.exp(scores - top)
    numer = jnp.einsum(
        "hqk,khd->hqd", expo.astype(jnp.bfloat16), values_all, preferred_element_type=jnp.float32
    )
    result = numer / jnp.sum(expo, axis=2)[..., None]
    return jnp.transpose(result, (1, 0, 2)).reshape(capacity, columns).astype(jnp.bfloat16)


def solution(mesh):
    in_specs = (P("seq", "tp"), P("seq", None, "tp"), P("seq"), P("seq"))
    out_specs = P("seq", "tp")
    return jax.shard_map(
        on_device, mesh=mesh, in_specs=in_specs, out_specs=out_specs, check_vma=False
    )
```

profile of v0, /device:TPU:0, one launch (start us, length us, event | category | flops | bytes accessed | tf_op | source)
XLA Modules:
  0.0 104.7 jit_solution(6532559039854450984)
XLA Ops:
  6.5 0.0 copy-start
  6.5 0.0 all-gather.3.cloned.1.call-start
  6.5 0.7 all-gather.3.cloned.1.call-update
  7.9 1.2 %dynamic-slice = u32[1]{0:T(128)} dynamic-slice(u32[32]{0:T(128)} %constant.83, u32[]{:T(128)S(6)} %add.147), dynamic_slice_sizes={1} | dynamic-slice | bytes 12
  9.1 0.7 dynamic-update-slice
  9.8 8.8 %all-reduce = s32[4]{0:T(128)S(1)} all-reduce(s32[4]{0:T(128)S(1)} %dynamic-update-slice), channel_id=2, replica_groups=mesh['seq'=4,'tp'=8] {'seq'}, use_global_device_ids=true, to_apply=%add | all-reduce | flops 4 | bytes 32
  18.6 3.5 %while.13 = (s32[]{:T(128)}, s32[1]{0:T(128)}, s32[]{:T(128)}, s32[4,1]{0,1:T(1,128)S(1)}, s32[]{:T(128)}) while((s32[]{:T(128)}, s32[1]{0:T(128)}, s32[]{:T(128)}, s32[4,1]{0,1:T(1,128)S(1)}, s32[]{:T(128)}) %tuple.38), condition=%wide.region_1.2_spmd, body=%wide.region_0.1_spmd.sunk | while | flops 5 | bytes 115 | solution.py:18
  18.6 0.6 constant_dynamic-slice_fusion.2
  19.8 0.6 constant_dynamic-slice_fusion.2
  21.0 0.6 constant_dynamic-slice_fusion.2
  22.2 0.1 compare_select_fusion.1
  22.2 0.1 reshape.223
  22.3 1.6 %gather_fusion = s32[128]{0:T(128)S(1)} fusion(s32[128]{0:T(128)} %param.8, s32[1024]{0:T(1024)S(1)} %pad_clamp_fusion.1), kind=kCustom, calls=%fused_computation | custom fusion | bytes 1536 | tf_op jit(solution)/shard_map/gather | solution.py:40
  23.9 0.1 gather.9
  24.0 0.6 copy.17
  24.6 3.2 %all-to-all-start = ((s32[4,32,2]{1,2,0:T(2,128)}), s32[4,32,2]{1,2,0:T(2,128)S(1)}, u32[]{:S(2)}, u32[]{:S(2)}) async-start(s32[4,32,2]{1,2,0:T(2,128)} %copy.17), calls=%async_computation | async-start | bytes 8192 | tf_op jit(solution)/shard_map/all_to_all | solution.py:47
  27.9 0.1 reshape.231
  28.0 0.0 copy-done
  28.0 0.8 gather_fusion.1
  28.8 0.1 add_compare_fusion.1
  28.9 0.7 broadcast_select_fusion
  30.2 2.5 %all-to-all-done = s32[4,32,2]{1,2,0:T(2,128)S(1)} async-done(((s32[4,32,2]{1,2,0:T(2,128)}), s32[4,32,2]{1,2,0:T(2,128)S(1)}, u32[]{:S(2)}, u32[]{:S(2)}) %all-to-all-start) | async-done | bytes 1056 | tf_op jit(solution)/shard_map/all_to_all | solution.py:47
  32.7 3.3 %all-to-all-start.1 = ((bf16[4,32,512]{2,1,0:T(8,128)(2,1)}), bf16[4,32,512]{2,1,0:T(8,128)(2,1)S(1)}, u32[]{:S(2)}, u32[]{:S(2)}) async-start(bf16[4,32,512]{2,1,0:T(8,128)(2,1)} %broadcast_select_fusion), calls=%async_computation.1 | async-start | bytes 262144 | tf_op jit(solution)/shard_map/all_to_all | solution.py:46
  36.0 0.1 reshape.219
  36.1 1.0 scatter_custom_fusion
  37.1 0.2 dynamic-update-slice.1
  37.4 7.8 %all-reduce.1 = s32[256]{0:T(256)S(1)} all-reduce(s32[256]{0:T(256)S(1)} %dynamic-update-slice.1), channel_id=1, replica_groups=mesh['seq'=4,'tp'=8] {'seq'}, use_global_device_ids=true, to_apply=%add.1 | all-reduce | flops 256 | bytes 2048
  45.2 0.1 broadcast_compare_fusion
  45.3 0.0 all-to-all-done.1
  45.3 1.1 %scatter_custom_fusion.1 = bf16[64,512]{1,0:T(8,128)(2,1)S(1)} fusion(s32[128]{0:T(128)S(1)} %get-tuple-element.98, bf16[128,512]{1,0:T(8,128)(2,1)S(1)} %bitcast.50, bf16[]{:T(256)} %constant.77.clone.1), kind=kCustom, calls=%fused_computation.22 | custom fusion | bytes 65538 | tf_op jit(solution)/shard_map/scatter | solution.py:53
  46.4 15.2 %all_gather.21 = bf16[64,4096]{1,0:T(8,128)(2,1)S(1)} all-gather(bf16[64,512]{1,0:T(8,128)(2,1)S(1)} %scatter_custom_fusion.1), channel_id=1, replica_groups=mesh['seq'=4,'tp'=8] {'tp'}, dimensions={1}, use_global_device_ids=true | all-gather | bytes 589824 | tf_op jit(solution)/shard_map/all_gather | solution.py:55
  61.6 21.9 %all-gather.3.cloned.1.call-done = bf16[4096,3,256]{2,0,1:T(8,128)(2,1)} async-done(((bf16[1024,3,256]{2,0,1:T(8,128)(2,1)}), bf16[4096,3,256]{2,0,1:T(8,128)(2,1)}) %all-gather.3.cloned.1.call-update) | async-done | bytes 6291472 | tf_op jit(solution)/shard_map/all_gather | solution.py:56
  83.5 4.0 %convolution_convert_fusion = bf16[64,3,256]{2,0,1:T(8,128)(2,1)S(1)} fusion(bf16[4096,3,256]{2,0,1:T(8,128)(2,1)} %all-gather.3.cloned.1.call-done, bf16[64,4096]{1,0:T(8,128)(2,1)S(1)} %all_gather.21), kind=kOutput, calls=%fused_computation.5 | convolution fusion | flops 402702336 | bytes 6914048 | tf_op jit(solution)/shard_map/rd,dgc->rgc/dot_general | solution.py:58
  87.5 9.0 %all_gather.23 = bf16[256,2,256]{2,0,1:T(8,128)(2,1)S(1)} all-gather(bf16[64,2,256]{2,0,1:T(8,128)(2,1)S(1)} %slice.29), channel_id=1, replica_groups=mesh['seq'=4,'tp'=8] {'seq'}, dimensions={0}, use_global_device_ids=true | all-gather | bytes 327680 | tf_op jit(solution)/shard_map/all_gather | solution.py:65
  96.6 0.3 fusion.20
  96.8 0.2 fusion.7
  97.0 0.2 fusion.3
  97.2 0.6 copy.35
  (16 shorter events, 0.2 us)
Async XLA Ops:
  6.5 21.5 %copy-start = (bf16[256,512]{1,0:T(8,128)(2,1)S(1)}, bf16[256,512]{1,0:T(8,128)(2,1)}, u32[]{:S(2)}) copy-start(bf16[256,512]{1,0:T(8,128)(2,1)} %param.6) | copy-start | bytes 786436
  6.5 76.9 %all-gather.3.cloned.1.call-start = ((), (), s32[]{:S(2)}) async-start(), calls=%async_computation.2 | async-start | bytes 7864320 | tf_op jit(solution)/shard_map/all_gather | solution.py:56
  24.6 8.0 %all-to-all-start = ((s32[4,32,2]{1,2,0:T(2,128)}), s32[4,32,2]{1,2,0:T(2,128)S(1)}, u32[]{:S(2)}, u32[]{:S(2)}) async-start(s32[4,32,2]{1,2,0:T(2,128)} %copy.17), calls=%async_computation | async-start | bytes 8192 | tf_op jit(solution)/shard_map/all_to_all | solution.py:47
  32.7 12.6 %all-to-all-start.1 = ((bf16[4,32,512]{2,1,0:T(8,128)(2,1)}), bf16[4,32,512]{2,1,0:T(8,128)(2,1)S(1)}, u32[]{:S(2)}, u32[]{:S(2)}) async-start(bf16[4,32,512]{2,1,0:T(8,128)(2,1)} %broadcast_select_fusion), calls=%async_computation.1 | async-start | bytes 262144 | tf_op jit(solution)/shard_map/all_to_all | solution.py:46
Sparse Core Ops, SparseCore 0:
  9.2 74.2 all-gather.2
where the time goes:
time: 105 us
  blocking collectives  40.9 us (39%)
  waiting for transfers between devices  25 us (24%)
  between operations  14.7 us (14%)
  local copies, waits for them, and re-layouts  10 us (10%)
  starting transfers between devices  6.57 us (6%)
  matrix products  4.44 us (4%)
  loops' own time  1.78 us (2%)
  other arithmetic  1.21 us (1%)
    all_gather x1, waiting for transfers between devices, on_device(): piece = lax.all_gather(w_qkv, 'seq', axis=0, tiled=True)  21.9 us
    unnamed x2, blocking collectives  16.7 us
    all_gather x1, blocking collectives, on_device(): full_rows = lax.all_gather(kept, 'tp', axis=1, tiled=True)  15.2 us
    all_gather x1, blocking collectives, on_device(): lax.all_gather(key_values, 'seq', axis=0, tiled=True)  9.02 us
    dot_general x1, matrix products, on_device(): jnp.einsum('rd,dgc->rgc', part_rows, piece, preferred_element_type=jnp.fl...  3.97 us
    all_to_all x1, starting transfers between devices, on_device(): lax.all_to_all(picked, 'seq', split_axis=0, concat_axis=0, tiled=True)  3.32 us
    all_to_all x1, starting transfers between devices, on_device(): lax.all_to_all(meta, 'seq', split_axis=0, concat_axis=0, tiled=True)  3.25 us
    all_to_all x1, waiting for transfers between devices, on_device(): lax.all_to_all(meta, 'seq', split_axis=0, concat_axis=0, tiled=True)  2.48 us
  transfers between devices with their start and end apart: 3, of which 2 were waited for; matrix products, arithmetic and copies ran while one was open for 10% of the time, Pallas kernels for 0%

commit v1 on v0

--- a/solution.py
+++ b/solution.py
@@ -4,6 +4,17 @@
 from jax.sharding import PartitionSpec as P
 
 HD = 128
+
+
+def pass_along(x, axis, dim):
+    size = lax.axis_size(axis)
+    right = [(i, (i + 1) % size) for i in range(size)]
+    parts = [x]
+    for reach in range(1, size):
+        parts = [lax.ppermute(parts[0], axis, right), *parts]
+    result = jnp.concatenate(parts, axis=dim)
+    turn = (lax.axis_index(axis) + 1) * parts[-1].shape[dim]
+    return jnp.roll(result, turn, axis=dim)
 
 
 def entering(value, axis, join, neutral):
@@ -53,7 +64,7 @@
     kept = jnp.zeros((capacity, flat.shape[1]), flat.dtype).at[target].set(flat, mode="drop")
     kept_pos = jnp.zeros((capacity,), jnp.int32).at[target].set(arrived_meta[:, 0], mode="drop")
     full_rows = lax.all_gather(kept, "tp", axis=1, tiled=True)
-    piece = lax.all_gather(w_qkv, "seq", axis=0, tiled=True)
+    piece = pass_along(w_qkv, "seq", 0)
     part_rows = lax.slice_in_dim(full_rows, 0, piece.shape[0], axis=1)
     projected = jnp.einsum(
         "rd,dgc->rgc", part_rows, piece, preferred_element_type=jnp.float32

time: 105 us -> 168 us (1.60)
  waiting for transfers between devices: 25 us -> 64 us
  blocking collectives: 40.9 us -> 67.8 us
  between operations: 14.7 us -> 1.44 us
  local copies, waits for them, and re-layouts: 10 us -> 17.8 us
  starting transfers between devices: 6.57 us -> 11.2 us
  matrix products: 4.44 us -> 1.67 us
    ppermute x0 -> x3, waiting for transfers between devices: none -> 35.6 us  [pass_along(): parts = [lax.ppermute(parts[0], axis, right), *parts]]
    unnamed x2, blocking collectives: 16.7 us -> 43.8 us
    all_to_all x1, waiting for transfers between devices: 2.48 us -> 28.4 us  [on_device(): lax.all_to_all(meta, 'seq', split_axis=0, concat_axis=0, tiled=True)]
    all_gather x1 -> x0, waiting for transfers between devices: 21.9 us -> none  [on_device(): piece = lax.all_gather(w_qkv, 'seq', axis=0, tiled=True)]
    unnamed x7 -> x22, local copies, waits for them, and re-layouts: 2.12 us -> 9.43 us
    ppermute x0 -> x3, starting transfers between devices: none -> 4.33 us  [pass_along(): parts = [lax.ppermute(parts[0], axis, right), *parts]]
    dot_general x1, matrix products: 3.97 us -> 1.2 us  [on_device(): jnp.einsum('rd,dgc->rgc', part_rows, piece, preferred_element_type=jnp.fl...]
  transfers between devices with their start and end apart: 3 -> 5, of which waited for: 2 -> 2; matrix products, arithmetic and copies ran while one was open for 10% -> 7% of each run, Pallas kernels for 0% -> 0%
where the time goes in v1:
time: 168 us
  blocking collectives  67.8 us (40%)
  waiting for transfers between devices  64 us (38%)
  local copies, waits for them, and re-layouts  17.8 us (11%)
  starting transfers between devices  11.2 us (7%)
  other arithmetic  1.88 us (1%)
  loops' own time  1.75 us (1%)
    unnamed x2, blocking collectives  43.8 us
    ppermute x3, waiting for transfers between devices, pass_along(): parts = [lax.ppermute(parts[0], axis, right), *parts]  35.6 us
    all_to_all x1, waiting for transfers between devices, on_device(): lax.all_to_all(meta, 'seq', split_axis=0, concat_axis=0, tiled=True)  28.4 us
    all_gather x1, blocking collectives, on_device(): full_rows = lax.all_gather(kept, 'tp', axis=1, tiled=True)  15.1 us
    unnamed x22, local copies, waits for them, and re-layouts  9.43 us
    all_gather x1, blocking collectives, on_device(): lax.all_gather(key_values, 'seq', axis=0, tiled=True)  8.94 us
    ppermute x3, starting transfers between devices, pass_along(): parts = [lax.ppermute(parts[0], axis, right), *parts]  4.33 us
    all_to_all x1, starting transfers between devices, on_device(): lax.all_to_all(meta, 'seq', split_axis=0, concat_axis=0, tiled=True)  3.59 us
  transfers between devices with their start and end apart: 5, of which 2 were waited for; matrix products, arithmetic and copies ran while one was open for 7% of the time, Pallas kernels for 0%

profile of v1, /device:TPU:0, one launch (start us, length us, event | category | flops | bytes accessed | tf_op | source)
XLA Modules:
  0.0 167.6 jit_solution(789960584681349484)
XLA Ops:
  0.0 3.0 %collective-permute-start = (bf16[1024,3,256]{2,0,1:T(8,128)(2,1)}, bf16[1024,3,256]{2,0,1:T(8,128)(2,1)S(1)}, u32[]{:S(2)}, u32[]{:S(2)}) collective-permute-start(bf16[1024,3,256]{2,0,1:T(8,128)(2,1)} %param.7), channel_id=1, source_target_pairs={{0,8},{8,16},{16,24},{24,0},{1,9},{9,17},{17,25},{25,1},{2,10},{10... | collective-permute-start | bytes 4718600 | tf_op jit(solution)/shard_map/ppermute | solution.py:14
  3.0 35.6 %collective-permute-done = bf16[1024,3,256]{2,0,1:T(8,128)(2,1)S(1)} collective-permute-done((bf16[1024,3,256]{2,0,1:T(8,128)(2,1)}, bf16[1024,3,256]{2,0,1:T(8,128)(2,1)S(1)}, u32[]{:S(2)}, u32[]{:S(2)}) %collective-permute-start) | collective-permute-done | bytes 1572896 | tf_op jit(solution)/shard_map/ppermute | solution.py:14
  38.6 0.8 collective-permute-start.1
  40.0 1.2 dynamic-slice
  41.2 0.7 dynamic-update-slice
  41.9 35.4 %all-reduce = s32[4]{0:T(128)S(1)} all-reduce(s32[4]{0:T(128)S(1)} %dynamic-update-slice), channel_id=2, replica_groups=mesh['seq'=4,'tp'=8] {'seq'}, use_global_device_ids=true, to_apply=%add | all-reduce | flops 4 | bytes 32
  77.3 3.5 %while.13 = (s32[]{:T(128)}, s32[1]{0:T(128)}, s32[]{:T(128)}, s32[4,1]{0,1:T(1,128)S(1)}, s32[]{:T(128)}) while((s32[]{:T(128)}, s32[1]{0:T(128)}, s32[]{:T(128)}, s32[4,1]{0,1:T(1,128)S(1)}, s32[]{:T(128)}) %tuple.36), condition=%wide.region_1.2_spmd, body=%wide.region_0.1_spmd.sunk | while | flops 5 | bytes 115 | solution.py:29
  77.3 0.6 constant_dynamic-slice_fusion.2
  78.4 0.6 constant_dynamic-slice_fusion.2
  79.6 0.6 constant_dynamic-slice_fusion.2
  80.8 0.1 compare_select_fusion.1
  80.9 0.1 reshape.223
  81.0 1.6 gather_fusion
  82.6 0.1 gather.9
  82.6 0.0 collective-permute-done.1
  82.6 0.6 collective-permute-start.2
  83.3 0.6 copy.17
  83.9 3.6 %all-to-all-start = ((s32[4,32,2]{1,2,0:T(2,128)}), s32[4,32,2]{1,2,0:T(2,128)S(1)}, u32[]{:S(2)}, u32[]{:S(2)}) async-start(s32[4,32,2]{1,2,0:T(2,128)} %copy.17), calls=%async_computation | async-start | bytes 8192 | tf_op jit(solution)/shard_map/all_to_all | solution.py:58
  87.5 0.1 reshape.231
  87.6 0.8 gather_fusion.1
  88.4 0.1 add_compare_fusion.1
  88.5 0.7 broadcast_select_fusion
  89.8 28.4 %all-to-all-done = s32[4,32,2]{1,2,0:T(2,128)S(1)} async-done(((s32[4,32,2]{1,2,0:T(2,128)}), s32[4,32,2]{1,2,0:T(2,128)S(1)}, u32[]{:S(2)}, u32[]{:S(2)}) %all-to-all-start) | async-done | bytes 1056 | tf_op jit(solution)/shard_map/all_to_all | solution.py:58
  118.2 3.3 %all-to-all-start.1 = ((bf16[4,32,512]{2,1,0:T(8,128)(2,1)}), bf16[4,32,512]{2,1,0:T(8,128)(2,1)S(1)}, u32[]{:S(2)}, u32[]{:S(2)}) async-start(bf16[4,32,512]{2,1,0:T(8,128)(2,1)} %broadcast_select_fusion), calls=%async_computation.1 | async-start | bytes 262144 | tf_op jit(solution)/shard_map/all_to_all | solution.py:57
  121.6 0.1 reshape.219
  121.7 1.0 scatter_custom_fusion
  122.7 0.2 dynamic-update-slice.1
  122.9 0.3 copy-done.3
  123.2 8.4 %all-reduce.1 = s32[256]{0:T(256)} all-reduce(s32[256]{0:T(256)S(1)} %dynamic-update-slice.1), channel_id=1, replica_groups=mesh['seq'=4,'tp'=8] {'seq'}, use_global_device_ids=true, to_apply=%add.1 | all-reduce | flops 256 | bytes 2048
  131.6 0.8 broadcast_compare_fusion
  132.4 0.0 all-to-all-done.1
  132.4 0.6 copy-done.2
  133.0 1.4 scatter_custom_fusion.1
  134.5 15.1 %all_gather.18 = bf16[64,4096]{1,0:T(8,128)(2,1)S(1)} all-gather(bf16[64,512]{1,0:T(8,128)(2,1)S(1)} %scatter_custom_fusion.1), channel_id=1, replica_groups=mesh['seq'=4,'tp'=8] {'tp'}, dimensions={1}, use_global_device_ids=true | all-gather | bytes 589824 | tf_op jit(solution)/shard_map/all_gather | solution.py:66
  149.5 1.5 constant_dynamic-update-slice_fusion.7
  151.0 1.5 constant_dynamic-update-slice_fusion.6
  152.5 0.1 constant_dynamic-update-slice_fusion.5
  152.7 0.1 constant_dynamic-update-slice_fusion.4
  152.8 1.5 constant_dynamic-update-slice_fusion.3
  154.3 1.5 constant_dynamic-update-slice_fusion.2
  155.8 0.1 constant_dynamic-update-slice_fusion.1
  155.9 0.1 constant_dynamic-update-slice_fusion
  156.0 1.2 fusion.2
  157.3 8.9 %all_gather.19 = bf16[256,2,256]{2,0,1:T(8,128)(2,1)S(1)} all-gather(bf16[64,2,256]{2,0,1:T(8,128)(2,1)S(1)} %slice.29), channel_id=1, replica_groups=mesh['seq'=4,'tp'=8] {'seq'}, dimensions={0}, use_global_device_ids=true | all-gather | bytes 327680 | tf_op jit(solution)/shard_map/all_gather | solution.py:76
  166.3 0.2 fusion.26
  166.6 0.2 fusion.12
  166.8 0.2 fusion.8
  167.0 0.6 copy.35
  (25 shorter events, 0.2 us)
Async XLA Ops:
  0.0 87.6 %copy-start = (bf16[256,512]{1,0:T(8,128)(2,1)S(1)}, bf16[256,512]{1,0:T(8,128)(2,1)}, u32[]{:S(2)}) copy-start(bf16[256,512]{1,0:T(8,128)(2,1)} %param.6) | copy-start | bytes 786436
  0.0 152.6 %copy-start.1 = (bf16[1024,3,256]{2,0,1:T(8,128)(2,1)S(1)}, bf16[1024,3,256]{2,0,1:T(8,128)(2,1)}, u32[]{:S(2)}) copy-start(bf16[1024,3,256]{2,0,1:T(8,128)(2,1)} %param.7) | copy-start | bytes 4718596
  0.0 38.6 %collective-permute-start = (bf16[1024,3,256]{2,0,1:T(8,128)(2,1)}, bf16[1024,3,256]{2,0,1:T(8,128)(2,1)S(1)}, u32[]{:S(2)}, u32[]{:S(2)}) collective-permute-start(bf16[1024,3,256]{2,0,1:T(8,128)(2,1)} %param.7), channel_id=1, source_target_pairs={{0,8},{8,16},{16,24},{24,0},{1,9},{9,17},{17,25},{25,1},{2,10},{10... | collective-permute-start | bytes 4718600 | tf_op jit(solution)/shard_map/ppermute | solution.py:14
  38.6 44.1 %collective-permute-start.1 = (bf16[1024,3,256]{2,0,1:T(8,128)(2,1)S(1)}, bf16[1024,3,256]{2,0,1:T(8,128)(2,1)}, u32[]{:S(2)}, u32[]{:S(2)}) collective-permute-start(bf16[1024,3,256]{2,0,1:T(8,128)(2,1)S(1)} %collective-permute-done), channel_id=1, source_target_pairs={{0,8},{8,16},{16,24},{24,0},{1,9},{9,17},{17,25},{25,1},{2,10},{10... | collective-permute-start | bytes 4718600 | tf_op jit(solution)/shard_map/ppermute | solution.py:14
  82.6 66.9 %collective-permute-start.2 = (bf16[1024,3,256]{2,0,1:T(8,128)(2,1)}, bf16[1024,3,256]{2,0,1:T(8,128)(2,1)}, u32[]{:S(2)}, u32[]{:S(2)}) collective-permute-start(bf16[1024,3,256]{2,0,1:T(8,128)(2,1)} %collective-permute-done.1), channel_id=1, source_target_pairs={{0,8},{8,16},{16,24},{24,0},{1,9},{9,17},{17,25},{25,1},{2,10},{10... | collective-permute-start | bytes 4718600 | tf_op jit(solution)/shard_map/ppermute | solution.py:14
  83.9 34.4 %all-to-all-start = ((s32[4,32,2]{1,2,0:T(2,128)}), s32[4,32,2]{1,2,0:T(2,128)S(1)}, u32[]{:S(2)}, u32[]{:S(2)}) async-start(s32[4,32,2]{1,2,0:T(2,128)} %copy.17), calls=%async_computation | async-start | bytes 8192 | tf_op jit(solution)/shard_map/all_to_all | solution.py:58
  118.2 14.1 %all-to-all-start.1 = ((bf16[4,32,512]{2,1,0:T(8,128)(2,1)}), bf16[4,32,512]{2,1,0:T(8,128)(2,1)S(1)}, u32[]{:S(2)}, u32[]{:S(2)}) async-start(bf16[4,32,512]{2,1,0:T(8,128)(2,1)} %broadcast_select_fusion), calls=%async_computation.1 | async-start | bytes 262144 | tf_op jit(solution)/shard_map/all_to_all | solution.py:57
  121.7 1.0 copy-start.4
  122.7 0.5 copy-start.3
  132.4 0.6 copy-start.2
